TPU v7x, 1024 devices: a whole 8x8x8 slice. The times are simulated.
1024 devices in a mesh: island: 32 (over x_hi, z), tp: 32 (over y, x_lo, core).
Axes of the slice: x: 8 (x_hi: 4, x_lo: 2; x = x_hi * 2 + x_lo), y: 8, z: 8, core: 2. Of those that a mesh axis runs over, the one named last changes fastest.
Arguments:
- residual: bfloat16 [32, 256, 4096], P('island', 'tp'), may hold values from -4 to 4
- gate_pre: bfloat16 [32, 256, 7168], P('island', None, 'tp'), may hold values from -9 to 9
- up_pre: bfloat16 [32, 256, 7168], P('island', None, 'tp'), may hold values from -9 to 9
- down_weight: bfloat16 [7168, 4096], P('tp'), may hold values from -0.0625 to 0.0625
- cotangent: bfloat16 [32, 256, 4096], P('island', 'tp'), may hold values from -1.5 to 1.5
- outer_weights: float32 [32, 262144], P('island', 'tp'), may hold values from -6 to 6
- deltas: float32 [32, 262144], P('island', 'tp'), may hold values from -6 to 6
- momentum: float32 [32, 262144], P('island', 'tp'), may hold values from -6 to 6
- partner: int32 [32], replicated, may hold values from 0 to 31, as said below
Outputs:
- mixed: bfloat16 [32, 256, 4096], P('island', 'tp')
- grad_gate: bfloat16 [32, 256, 7168], P('island', None, 'tp')
- grad_up: bfloat16 [32, 256, 7168], P('island', None, 'tp')
- grad_down: bfloat16 [32, 7168, 4096], P('island', 'tp')
- new_outer: float32 [32, 262144], P('island', 'tp')
- new_momentum: float32 [32, 262144], P('island', 'tp')
Inputs may be any that keep to these rules, and one draw needn't show every extreme that they name: Islands come in pairs: partner[partner[i]] = i and partner[i] != i for every island i.
All inputs are finite; a program needn't handle non-finite values.
Results may differ from a plain program's by a relative error of at most 0.023.
Values may be sent and summed in bfloat16 or wider, within the bound.
A program may use at most 32 MiB of HBM per device.

v0:
```python
import jax
import jax.numpy as jnp
from jax import lax
from jax.sharding import Mesh
from jax.sharding import PartitionSpec as P

ISLAND = ("island_0", "island_1")


decay_rate = 0.5
delta_rate = 0.7
pull_rate = 0.6


def split_up(value, dim, size):
    lengths = value.shape
    parts = value.reshape(*lengths[:dim], size, lengths[dim] // size, *lengths[dim + 1 :])
    return jnp.moveaxis(parts, dim, 0)


def summed_on_arrival(value, axis, dim):
    parts = split_up(value, dim, lax.axis_size(axis))
    arrived = lax.all_to_all(parts, axis, split_axis=0, concat_axis=0, tiled=True)
    return arrived.astype(jnp.float32).sum(axis=0)


def piece_ends(length, count):
    unit = 8 if length >= 8 * count else 1
    return [length // unit * k // count * unit for k in range(1, count)]


def stacked_from(value, axes, sequence):
    parts = value
    for k in sequence:
        parts = lax.all_gather(parts, axes[k])
    done = sequence[::-1]
    back = [done.index(k) for k in range(len(axes))]
    parts = parts.transpose(*back, *range(len(axes), parts.ndim))
    return parts.reshape(-1, *value.shape)


def in_order(parts, dim):
    lengths = list(parts.shape[1:])
    lengths[dim] *= parts.shape[0]
    return jnp.moveaxis(parts, 0, dim).reshape(lengths)


def gather_at_once(value, axes, dim):
    split_at = max(range(max(1, value.ndim - 1)), key=lambda d: value.shape[d])
    count, finished = (len(axes), [])
    for first, section in enumerate(
        jnp.split(value, piece_ends(value.shape[split_at], count), axis=split_at)
    ):
        if section.size:
            sequence = [(first - k) % count for k in range(count)]
            finished.append(stacked_from(section, axes, sequence))
    return in_order(jnp.concatenate(finished, axis=split_at + 1), dim)


def per_device(
    residual, gate_pre, up_pre, down_weight, cotangent, outer_weights, deltas, momentum, partner
):
    residual = residual[0]
    gate_pre = gate_pre[0]
    up_pre = up_pre[0]
    cotangent = cotangent[0]
    gate_value = gate_pre.astype(jnp.float32)
    up_value = up_pre.astype(jnp.float32)
    logistic = jax.nn.sigmoid(gate_value)
    activated = gate_value * logistic
    hidden = (activated * up_value).astype(jnp.bfloat16)
    rows_hidden = hidden
    summed = summed_on_arrival(
        jnp.dot(rows_hidden, down_weight, preferred_element_type=jnp.float32).astype(jnp.bfloat16),
        "tp",
        0,
    )
    mixed = (residual.astype(jnp.float32) + summed).astype(jnp.bfloat16)
    piece = lax.all_gather(cotangent, "tp", axis=0, tiled=True)
    rows_hidden = hidden
    weight_total = lax.dot_general(
        rows_hidden, piece, (((0,), (0,)), ((), ())), preferred_element_type=jnp.float32
    )
    block_grad = lax.dot_general(
        piece, down_weight, (((1,), (1,)), ((), ())), preferred_element_type=jnp.float32
    )
    weight_total, grad_hidden = (weight_total, block_grad)
    grad_down = weight_total.astype(jnp.bfloat16)
    slope = logistic * (1.0 + gate_value * (1.0 - logistic))
    grad_gate = (grad_hidden * up_value * slope).astype(jnp.bfloat16)
    grad_up = (grad_hidden * activated).astype(jnp.bfloat16)
    island_count = lax.axis_size(ISLAND)
    own_island = lax.axis_index(ISLAND)
    numbers = jnp.arange(island_count, dtype=jnp.int32)
    partner_index = jnp.sum(jnp.where(numbers == own_island, partner, 0))
    payload = (0.5 * delta_rate * deltas + 0.5 * pull_rate * outer_weights)[None]
    piece = gather_at_once(payload.astype(jnp.bfloat16), ISLAND, 1).astype(jnp.float32)
    count_rows = piece.shape[1]
    chosen = (jnp.arange(count_rows, dtype=jnp.int32) == partner_index).astype(jnp.float32)
    received = jnp.zeros_like(payload) + jnp.sum(
        piece * chosen[None, :, None], axis=1, keepdims=True
    )
    new_momentum = (
        decay_rate * momentum
        + 0.5 * delta_rate * deltas
        - 0.5 * pull_rate * outer_weights
        + received[0]
    )
    new_outer = outer_weights + new_momentum
    return (mixed[None], grad_gate[None], grad_up[None], grad_down[None], new_outer, new_momentum)


def solution(mesh):
    torus = Mesh(mesh.devices.reshape(4, 8, mesh.shape["tp"]), ("island_0", "island_1", "tp"))
    placed = (
        P(ISLAND, "tp", None),
        P(ISLAND, None, "tp"),
        P(ISLAND, None, "tp"),
        P("tp", None),
        P(ISLAND, "tp", None),
        P(ISLAND, "tp"),
        P(ISLAND, "tp"),
        P(ISLAND, "tp"),
        P(),
    )
    return jax.shard_map(
        per_device,
        mesh=torus,
        in_specs=placed,
        out_specs=(
            P(ISLAND, "tp", None),
            P(ISLAND, None, "tp"),
            P(ISLAND, None, "tp"),
            P(ISLAND, "tp", None),
            P(ISLAND, "tp"),
            P(ISLAND, "tp"),
        ),
        check_vma=False,
    )
```

profile of v0, /device:TPU:1, one launch (start us, length us, event | category | flops | bytes accessed | tf_op | source)
XLA Modules:
  0.0 132.0 jit_solution(8951794720233339042)
XLA Ops:
  7.2 0.0 copy-start
  7.2 1.5 %copy-done = bf16[224,4096]{1,0:T(8,128)(2,1)S(1)} copy-done((bf16[224,4096]{1,0:T(8,128)(2,1)S(1)}, bf16[224,4096]{1,0:T(8,128)(2,1)}, u32[]{:S(2)}) %copy-start) | copy-done | bytes 1835032
  8.7 3.0 %fusion = bf16[32,8,4096]{2,1,0:T(8,128)(2,1)} fusion(bf16[224,4096]{1,0:T(8,128)(2,1)S(1)} %copy-done, bf16[1,256,224]{1,2,0:T(8,128)(2,1)} %param.11, bf16[1,256,224]{1,2,0:T(8,128)(2,1)} %param.10), kind=kOutput, calls=%fused_computation.2 | convolution fusion | flops 471269376 | bytes 4161536 | tf_op jit(solution)/shard_map/dot_general | solution.py:74
  11.7 0.0 copy-start.4
  11.7 0.0 copy-start.5
  11.7 0.0 copy-start.8
  11.7 0.0 copy-start.7
  11.7 18.6 %all-to-all-start = ((bf16[32,8,4096]{2,1,0:T(8,128)(2,1)}), bf16[32,8,4096]{2,1,0:T(8,128)(2,1)}, u32[]{:S(2)}, u32[]{:S(2)}) async-start(bf16[32,8,4096]{2,1,0:T(8,128)(2,1)} %fusion), calls=%async_computation | async-start | bytes 4194304 | tf_op jit(solution)/shard_map/all_to_all | solution.py:23
  30.3 0.0 all-gather.6.cloned.1.call-start
  30.4 0.7 all-gather.6.cloned.1.call-update
  31.1 0.0 copy-done.4
  31.1 0.0 copy-done.5
  31.1 0.1 convert_bitcast_fusion
  31.2 25.0 %all-gather.3 = bf16[8,1,8192]{2,1,0:T(2,128)(2,1)S(1)} all-gather(bf16[1,1,8192]{2,1,0:T(2,128)(2,1)S(1)} %convert_bitcast_fusion), channel_id=3, replica_groups=mesh['island_0'=4,'island_1'=8,'tp'=32] {'island_1'}, dimensions={0}, use_global_device_ids=true | all-gather | bytes 147456 | tf_op jit(solution)/shard_map/all_gather | solution.py:35
  56.2 0.0 copy-start.6
  56.2 0.0 copy-start.2
  56.2 0.0 copy-start.3
  56.2 0.1 copy.17
  56.3 0.0 copy-done.8
  56.4 0.6 fusion.17
  57.0 0.6 compare_convert_fusion
  57.6 15.5 %all-gather.2 = bf16[32,8192]{1,0:T(8,128)(2,1)S(1)} all-gather(bf16[8,8192]{1,0:T(8,128)(2,1)S(1)} %bitcast.50), channel_id=4, replica_groups=mesh['island_0'=4,'island_1'=8,'tp'=32] {'island_0'}, dimensions={0}, use_global_device_ids=true | all-gather | bytes 655360 | tf_op jit(solution)/shard_map/all_gather | solution.py:35
  73.1 0.2 fusion.5
  73.4 0.0 copy-done.7
  73.4 0.7 fusion.20
  74.1 15.5 %all-to-all-done = bf16[32,8,4096]{2,1,0:T(8,128)(2,1)} async-done(((bf16[32,8,4096]{2,1,0:T(8,128)(2,1)}), bf16[32,8,4096]{2,1,0:T(8,128)(2,1)}, u32[]{:S(2)}, u32[]{:S(2)}) %all-to-all-start) | async-done | bytes 2097184 | tf_op jit(solution)/shard_map/all_to_all | solution.py:23
  89.6 1.9 %convert_reduce_fusion = f32[8,4096]{1,0:T(8,128)S(1)} fusion(bf16[32,8,4096]{2,1,0:T(8,128)(2,1)} %all-to-all-done), kind=kLoop, calls=%fused_computation.4 | loop fusion | flops 2064384 | bytes 2228224 | tf_op jit(solution)/shard_map/reduce_sum | solution.py:24
  91.5 0.0 copy-done.6
  91.5 0.6 fusion.14
  92.1 27.9 %all-gather.6.cloned.1.call-done = bf16[1,256,4096]{2,1,0:T(8,128)(2,1)} async-done(((bf16[1,8,4096]{2,1,0:T(8,128)(2,1)}), bf16[1,256,4096]{2,1,0:T(8,128)(2,1)}) %all-gather.6.cloned.1.call-update) | async-done | bytes 2097168 | tf_op jit(solution)/shard_map/all_gather | solution.py:79
  120.1 0.0 copy-done.2
  120.1 0.0 copy-done.3
  120.1 0.0 copy-start.1
  120.1 3.2 %fusion.15 = (bf16[1,256,224]{1,2,0:T(8,128)(2,1)}, bf16[1,256,224]{1,2,0:T(8,128)(2,1)}) fusion(bf16[1,256,224]{1,2,0:T(8,128)(2,1)S(1)} %copy-done.3, bf16[1,256,224]{1,2,0:T(8,128)(2,1)S(1)} %copy-done.2, bf16[224,4096]{1,0:T(8,128)(2,1)S(1)} %copy-done, bf16[1,256,4096]{2,1,0:T(8,128)(2,1)} %all-gather.6.cloned.1.call-done), kind=kOutput, calls=%fused_computation.27 | convolution fusion | flops 470622208 | bytes 4390912 | tf_op jit(solution)/shard_map/dot_general | solution.py:84
  123.3 0.0 copy-done.1
  123.3 1.9 %fusion.1 = bf16[1,224,4096]{2,1,0:T(8,128)(2,1)} fusion(bf16[1,256,4096]{2,1,0:T(8,128)(2,1)S(1)} %copy-done.1, bf16[1,256,224]{1,2,0:T(8,128)(2,1)S(1)} %copy-done.2, bf16[1,256,224]{1,2,0:T(8,128)(2,1)S(1)} %copy-done.3), kind=kOutput, calls=%fused_computation.3 | convolution fusion | flops 471138304 | bytes 4161536 | tf_op jit(solution)/shard_map/dot_general | solution.py:81
Async XLA Ops:
  7.2 1.5 %copy-start = (bf16[224,4096]{1,0:T(8,128)(2,1)S(1)}, bf16[224,4096]{1,0:T(8,128)(2,1)}, u32[]{:S(2)}) copy-start(bf16[224,4096]{1,0:T(8,128)(2,1)} %param.12) | copy-start | bytes 5505028
  11.7 19.4 %copy-start.4 = (f32[1,8192]{1,0:T(1,128)S(1)}, f32[1,8192]{1,0:T(1,128)}, u32[]{:S(2)}) copy-start(f32[1,8192]{1,0:T(1,128)} %param.14) | copy-start | bytes 98308
  11.7 19.4 %copy-start.5 = (f32[1,8192]{1,0:T(1,128)S(1)}, f32[1,8192]{1,0:T(1,128)}, u32[]{:S(2)}) copy-start(f32[1,8192]{1,0:T(1,128)} %param.15) | copy-start | bytes 98308
  11.7 44.6 %copy-start.8 = (s32[32]{0:T(128)S(1)}, s32[32]{0:T(128)}, u32[]{:S(2)}) copy-start(s32[32]{0:T(128)} %param.17) | copy-start | bytes 388
  11.7 61.7 %copy-start.7 = (f32[1,8192]{1,0:T(1,128)S(1)}, f32[1,8192]{1,0:T(1,128)}, u32[]{:S(2)}) copy-start(f32[1,8192]{1,0:T(1,128)} %param.16) | copy-start | bytes 98308
  11.7 77.9 %all-to-all-start = ((bf16[32,8,4096]{2,1,0:T(8,128)(2,1)}), bf16[32,8,4096]{2,1,0:T(8,128)(2,1)}, u32[]{:S(2)}, u32[]{:S(2)}) async-start(bf16[32,8,4096]{2,1,0:T(8,128)(2,1)} %fusion), calls=%async_computation | async-start | bytes 4194304 | tf_op jit(solution)/shard_map/all_to_all | solution.py:23
  30.3 89.7 %all-gather.6.cloned.1.call-start = ((), (), s32[]{:S(2)}) async-start(), calls=%async_computation.1 | async-start | bytes 2162688 | tf_op jit(solution)/shard_map/all_gather | solution.py:79
  56.2 35.3 %copy-start.6 = (bf16[1,8,4096]{2,1,0:T(8,128)(2,1)S(1)}, bf16[1,8,4096]{2,1,0:T(8,128)(2,1)}, u32[]{:S(2)}) copy-start(bf16[1,8,4096]{2,1,0:T(8,128)(2,1)} %param.9) | copy-start | bytes 196612
  56.2 63.9 %copy-start.2 = (bf16[1,256,224]{1,2,0:T(8,128)(2,1)S(1)}, bf16[1,256,224]{1,2,0:T(8,128)(2,1)}, u32[]{:S(2)}) copy-start(bf16[1,256,224]{1,2,0:T(8,128)(2,1)} %param.11) | copy-start | bytes 344068
  56.2 63.9 %copy-start.3 = (bf16[1,256,224]{1,2,0:T(8,128)(2,1)S(1)}, bf16[1,256,224]{1,2,0:T(8,128)(2,1)}, u32[]{:S(2)}) copy-start(bf16[1,256,224]{1,2,0:T(8,128)(2,1)} %param.10) | copy-start | bytes 344068
  120.1 3.2 %copy-start.1 = (bf16[1,256,4096]{2,1,0:T(8,128)(2,1)S(1)}, bf16[1,256,4096]{2,1,0:T(8,128)(2,1)}, u32[]{:S(2)}) copy-start(bf16[1,256,4096]{2,1,0:T(8,128)(2,1)} %all-gather.6.cloned.1.call-done) | copy-start | bytes 6291460
Sparse Core Ops, SparseCore 0:
  33.9 86.1 all-gather.5
where the time goes:
time: 132 us
  waiting for transfers between devices  44.1 us (33%)
  blocking collectives  40.5 us (31%)
  starting transfers between devices  18.6 us (14%)
  between operations  14.1 us (11%)
  matrix products  8.17 us (6%)
  other arithmetic  4.85 us (4%)
  local copies, waits for them, and re-layouts  1.68 us (1%)
    all_gather x2, blocking collectives, stacked_from(): parts = lax.all_gather(parts, axes[k])  40.5 us
    all_gather x1, waiting for transfers between devices, per_device(): piece = lax.all_gather(cotangent, 'tp', axis=0, tiled=True)  27.9 us
    all_to_all x1, starting transfers between devices, summed_on_arrival(): lax.all_to_all(parts, axis, split_axis=0, concat_axis=0, tiled=True)  18.6 us
    all_to_all x1, waiting for transfers between devices, summed_on_arrival(): lax.all_to_all(parts, axis, split_axis=0, concat_axis=0, tiled=True)  15.5 us
    dot_general x1, matrix products, per_device(): lax.dot_general(piece, down_weight, (((1,), (1,)), ((), ())), preferred_e...  3.22 us
    dot_general x1, matrix products, per_device(): jnp.dot(rows_hidden, down_weight, preferred_element_type=jnp.float32)  3.05 us
  transfers between devices with their start and end apart: 2, of which 2 were waited for; matrix products, arithmetic and copies ran while one was open for 4% of the time, Pallas kernels for 0%

commit v1 on v0

v1 whole, which is shorter than its diff:
```python
import functools

import jax
import jax.numpy as jnp
from jax import lax
from jax.experimental import pallas as pl
from jax.experimental.pallas import tpu as pltpu
from jax.sharding import Mesh
from jax.sharding import PartitionSpec as P

MESH = pl.DeviceIdType.MESH
ISLAND = ("xh", "z")
TP = ("y", "xl", "c")

decay_rate = 0.5
delta_rate = 0.7
pull_rate = 0.6

F32 = jnp.float32
BF16 = jnp.bfloat16

RIGHT, LEFT = 0, 1
F_A, F_B, P_A = 0, 1, 2


class Links:
    def __init__(self, send_sem, recv_sem):
        self.send_sem, self.recv_sem = send_sem, recv_sem
        self.numbers, self.sent = {}, []

    def number(self, key):
        return self.numbers.setdefault(key, len(self.numbers))

    def make(self, key, src, dst, peer):
        k = self.number(key)
        return pltpu.make_async_remote_copy(
            src_ref=src,
            dst_ref=dst,
            send_sem=self.send_sem.at[k],
            recv_sem=self.recv_sem.at[k],
            device_id=peer,
            device_id_type=MESH,
        )

    def send(self, key, src, dst, peer):
        copy = self.make(key, src, dst, peer)
        copy.start()
        self.sent.append(copy)

    def arrive(self, key, dst, peer):
        self.make(key, dst, dst, peer).wait_recv()

    def drain(self):
        for copy in self.sent:
            copy.wait_send()


def message_count(ny, nz, nxh):
    return 4 * ny + 1 + ny + 3 * ny + 2 + ny + 1 + 3 * ny + nz + nxh + 8


def kernel(
    sizes,
    residual_hbm,
    gate_hbm,
    up_hbm,
    w_hbm,
    cot_hbm,
    outer_hbm,
    deltas_hbm,
    momentum_hbm,
    partner_hbm,
    mixed_hbm,
    grad_gate_hbm,
    grad_up_hbm,
    grad_down_hbm,
    new_outer_hbm,
    new_momentum_hbm,
    residual_v,
    gate_v,
    up_v,
    w_v,
    cot_v,
    outer_v,
    deltas_v,
    momentum_v,
    partner_s,
    hid_t,
    hid,
    act_v,
    slope_v,
    pmine,
    psend,
    precv,
    xsend,
    xrecv,
    ysend,
    yrecv,
    fsend,
    frecv,
    zbuf,
    hsend,
    hbuf,
    mixed_v,
    grad_gate_v,
    grad_up_v,
    grad_down_v,
    new_outer_v,
    new_momentum_v,
    load_sem,
    store_sem,
    send_sem,
    recv_sem,
):
    nxh, nz, ny = sizes
    far = ny // 2
    width = cot_v.shape[2]
    half, quarter = width // 2, width // 4
    ca, cb = pl.ds(0, half), pl.ds(half, half)
    q0, q1 = pl.ds(0, quarter), pl.ds(quarter, quarter)

    xh, z, y = lax.axis_index("xh"), lax.axis_index("z"), lax.axis_index("y")
    x, c = lax.axis_index("xl"), lax.axis_index("c")

    def at_y(k):
        return lax.rem(y + (k + ny), ny)

    def block(yy, xx):
        return (yy * 2 + xx) * 2 + c

    step_to = ({"y": at_y(1)}, {"y": at_y(-1)})
    sign = (1, -1)
    across = {"xl": 1 - x}
    sibling = {"c": 1 - c}

    loads = []

    def load(src, dst):
        copy = pltpu.make_async_copy(src, dst, load_sem.at[len(loads)])
        copy.start()
        loads.append(copy)
        return copy

    own = block(y, x)
    cot_in = load(cot_hbm, cot_v.at[own])
    gate_in = load(gate_hbm, gate_v)
    up_in = load(up_hbm, up_v)
    w_in = load(w_hbm, w_v)
    outer_in = load(outer_hbm, outer_v)
    deltas_in = load(deltas_hbm, deltas_v)
    momentum_in = load(momentum_hbm, momentum_v)
    partner_in = load(partner_hbm, partner_s)
    residual_in = load(residual_hbm, residual_v)

    peers = [step_to[0], step_to[1], across, sibling]
    for k in range(1, nz):
        peers.append({"z": lax.rem(z + k, nz)})
    for k in range(1, nxh):
        peers.append({"xh": lax.rem(xh + k, nxh)})
    barrier = pltpu.get_barrier_semaphore()
    for peer in peers:
        pl.semaphore_signal(barrier, inc=1, device_id=peer, device_id_type=MESH)
    gate_in.wait()
    up_in.wait()

    links = Links(send_sem, recv_sem)

    cot_in.wait()
    pl.semaphore_wait(barrier, len(peers))

    def ag_region(way, d, part, yy):
        ref = cot_v.at[block(yy, x if part == "f" else 1 - x)]
        if part == "f":
            if d < far:
                return ref
            return ref.at[:, ca if way == RIGHT else cb]
        if d < far:
            return ref.at[:, ca]
        return ref.at[:, q0 if way == RIGHT else q1]

    def ag_send(way, d, part):
        ref = ag_region(way, d, part, at_y(-sign[way] * (d - 1)))
        links.send(("ag", way, d, part), ref, ref, step_to[way])

    def ag_arrive(way, d, part):
        ref = ag_region(way, d, part, at_y(-sign[way] * d))
        links.arrive(("ag", way, d, part), ref, step_to[way])

    def hand(key, ref):
        links.send(("hand",) + key, ref, ref, sibling)

    def cross(k):
        ref = cot_v.at[block(at_y(k), x), :, cb]
        links.send(("cross", k % ny), ref, ref, across)

    def cross_arrive(k):
        ref = cot_v.at[block(at_y(k), 1 - x), :, cb]
        links.arrive(("cross", k % ny), ref, across)
        hand(("pb", k % ny), ref)

    ref = cot_v.at[own, :, ca]
    links.send(("cross_a",), ref, ref, across)
    ag_send(RIGHT, 1, "f")
    ag_send(LEFT, 1, "f")
    cross(0)
    hand(("f", 0), cot_v.at[own])

    outer_in.wait()
    deltas_in.wait()
    zbuf[z] = (0.5 * delta_rate * deltas_v[...] + 0.5 * pull_rate * outer_v[...]).astype(BF16)
    for k in range(1, nz):
        links.send(("z", k), zbuf.at[z], zbuf.at[z], {"z": lax.rem(z + k, nz)})

    gate = gate_v[...].astype(F32)
    up = up_v[...].astype(F32)
    logistic = jax.nn.sigmoid(gate)
    act = gate * logistic
    hidden = act * up
    hid_t[...] = hidden.astype(BF16)
    ff = hidden.shape[0]
    rows = hidden.T.reshape(ny, 2, 2, 8, ff)
    for cc in range(2):
        for xx in range(2):
            piece = rows[:, xx, cc].reshape(ny * 8, ff)
            hid[cc, pl.ds(xx * ny * 8, ny * 8), :] = piece.astype(BF16)
    w_in.wait()
    for part, cols in ((0, ca), (1, cb)):
        out = jnp.dot(hid[1 - c], w_v[:, cols], preferred_element_type=F32)
        psend[:, :, :, cols] = out.astype(BF16).reshape(2, ny, 8, half)
        links.send(("pair", part), psend.at[:, :, :, cols], precv.at[:, :, :, cols], sibling)

    ref = cot_v.at[block(y, 1 - x), :, ca]
    links.arrive(("cross_a",), ref, across)
    ag_send(RIGHT, 1, "p")
    ag_send(LEFT, 1, "p")
    hand(("pa", 0), ref)

    for part, cols in ((0, ca), (1, cb)):
        out = jnp.dot(hid[c], w_v[:, cols], preferred_element_type=F32)
        pmine[:, :, :, cols] = out.reshape(2, ny, 8, half)

    act_v[...] = act
    slope_v[...] = up * (logistic * (1.0 + gate * (1.0 - logistic)))

    def ag_step(d):
        for way in (RIGHT, LEFT):
            k = -sign[way] * d
            yy = at_y(k)
            ag_arrive(way, d, "f")
            if d < far:
                ag_send(way, d + 1, "f")
                cross(k)
                hand(("f", k % ny), cot_v.at[block(yy, x)])
            elif way == LEFT:
                cross(k)
                hand(("f", k % ny), cot_v.at[block(yy, x)])
            ag_arrive(way, d, "p")
            if d < far:
                ag_send(way, d + 1, "p")
                hand(("pa", k % ny), cot_v.at[block(yy, 1 - x), :, ca])
            elif way == LEFT:
                hand(("pa", k % ny), cot_v.at[block(yy, 1 - x), :, ca])

    def mine(xx, yy, cols):
        return pmine[xx, yy, :, cols] + precv[xx, yy, :, cols].astype(F32)

    def total_of(part, yy):
        if part == F_A:
            return mine(x, yy, ca)
        if part == F_B:
            return mine(x, yy, cb) + xrecv[yy].astype(F32)
        return mine(1 - x, yy, ca)

    def covered(way, part, d):
        if d < far:
            return pl.ds(0, half)
        if part == P_A:
            return q0 if way == RIGHT else q1
        return pl.ds(0, half) if (part == F_A) == (way == RIGHT) else None

    def rs_arrive(way, d, part):
        cols = covered(way, part, d)
        if cols is not None:
            links.arrive(("rs", way, d, part), yrecv.at[way, d - 1, part, :, cols], step_to[way])
        return cols

    def came(way, d, part, cols):
        got = yrecv[way, d - 1, part, :, cols].astype(F32)
        if cols.size == half:
            return got
        rest = jnp.zeros_like(got)
        return jnp.concatenate([got, rest] if cols.start == 0 else [rest, got], axis=1)

    def rs_send(way, d, part):
        cols = covered(way, part, d)
        if cols is None:
            return
        value = total_of(part, at_y(sign[way] * d))
        if d < far:
            before = rs_arrive(way, d + 1, part)
            if before is not None:
                value = value + came(way, d + 1, part, before)
        ysend[way, d - 1, part] = value.astype(BF16)
        links.send(
            ("rs", way, d, part),
            ysend.at[way, d - 1, part, :, cols],
            yrecv.at[way, d - 1, part, :, cols],
            step_to[way],
        )

    def x_send(k):
        yy = at_y(k)
        xsend[yy] = mine(1 - x, yy, cb).astype(BF16)
        links.send(("x", k % ny), xsend.at[yy], xrecv.at[yy], across)

    def x_arrive(k):
        yy = at_y(k)
        links.arrive(("x", k % ny), xrecv.at[yy], across)

    ag_step(1)

    cols = ca
    links.arrive(("pair", 0), precv.at[:, :, :, cols], sibling)
    for part in (F_A, P_A):
        for way in (RIGHT, LEFT):
            rs_send(way, far, part)
    rs_send(LEFT, far - 1, F_A)
    links.arrive(("pair", 1), precv.at[:, :, :, cb], sibling)
    order = [far]
    for d in range(far - 1, 0, -1):
        order += [d, -d]
    order.append(0)
    for k in order:
        x_send(k)

    partner_in.wait()
    for k in range(1, nz):
        src = lax.rem(z + (nz - k), nz)
        links.arrive(("z", k), zbuf.at[src], {"z": src})
    hbuf[xh] = zbuf[lax.rem(partner_s[xh * nz + z], nz)]
    for k in range(1, nxh):
        to = lax.rem(xh + k, nxh)
        hsend[k] = zbuf[lax.rem(partner_s[to * nz + z], nz)]
        links.send(("xh", k), hsend.at[k], hbuf.at[xh], {"xh": to})

    if far > 2:
        ag_step(2)
    x_arrive(far)
    rs_send(LEFT, far, F_B)
    x_arrive(far - 1)
    rs_send(RIGHT, far - 1, F_B)
    x_arrive(-(far - 1))

    cross_arrive(0)
    cross_seen = [0]

    def cross_more(d):
        for k in (d, -d):
            if k % ny not in cross_seen:
                cross_arrive(k)
                cross_seen.append(k % ny)

    rs_send(RIGHT, far - 1, F_A)
    for way in (RIGHT, LEFT):
        rs_send(way, far - 1, P_A)
    rs_send(LEFT, far - 1, F_B)
    cross_more(1)

    for d in range(far - 2, 0, -1):
        if far - d + 1 < far:
            ag_step(far - d + 1)
        for k in (d, -d):
            x_arrive(k)
        for part in (F_A, P_A, F_B):
            for way in (RIGHT, LEFT):
                rs_send(way, d, part)
        cross_more(far - d)
    ag_step(far)
    for d in range(2, far + 1):
        cross_more(d)

    momentum_in.wait()
    for k in range(1, nxh):
        src = lax.rem(xh + (nxh - k), nxh)
        links.arrive(("xh", k), hbuf.at[src], {"xh": src})
    received = hbuf[lax.div(partner_s[xh * nz + z], nz)].astype(F32)
    new_momentum = (
        decay_rate * momentum_v[...]
        + 0.5 * delta_rate * deltas_v[...]
        - 0.5 * pull_rate * outer_v[...]
        + received
    )
    new_momentum_v[...] = new_momentum
    new_outer_v[...] = outer_v[...] + new_momentum
    stores = []

    def store(src, dst):
        copy = pltpu.make_async_copy(src, dst, store_sem.at[len(stores)])
        copy.start()
        stores.append(copy)

    store(new_momentum_v, new_momentum_hbm)
    store(new_outer_v, new_outer_hbm)

    for way in (RIGHT, LEFT):
        rs_arrive(way, 1, P_A)
    value = total_of(P_A, y)
    for way in (RIGHT, LEFT):
        value = value + yrecv[way, 0, P_A].astype(F32)
    fsend[...] = value.astype(BF16)
    links.send(("last",), fsend, frecv, across)

    for k in range(ny):
        yy = at_y(k)
        theirs = (yy * 2 + x) * 2 + 1 - c
        other = (yy * 2 + 1 - x) * 2 + 1 - c
        links.arrive(("hand", "f", k), cot_v.at[theirs], sibling)
        links.arrive(("hand", "pa", k), cot_v.at[other, :, ca], sibling)
        links.arrive(("hand", "pb", k), cot_v.at[other, :, cb], sibling)

    tokens = cot_v.shape[0] * 8
    cot = cot_v[...].reshape(tokens, width)
    grad_hidden = lax.dot_general(
        w_v[...], cot, (((1,), (1,)), ((), ())), preferred_element_type=F32
    )
    grad_gate_v[...] = (grad_hidden * slope_v[...]).astype(BF16)
    grad_up_v[...] = (grad_hidden * act_v[...]).astype(BF16)
    store(grad_gate_v, grad_gate_hbm)
    store(grad_up_v, grad_up_hbm)
    for cols in (ca, cb):
        part = cot_v[:, :, cols].reshape(tokens, half)
        grad_down_v[:, cols] = jnp.dot(hid_t[...], part, preferred_element_type=F32).astype(BF16)
        store(grad_down_v.at[:, cols], grad_down_hbm.at[:, cols])

    residual_in.wait()
    x_arrive(0)
    for part, cols in ((F_A, ca), (F_B, cb)):
        value = total_of(part, y) + residual_v[:, cols].astype(F32)
        for way in (RIGHT, LEFT):
            rs_arrive(way, 1, part)
            value = value + yrecv[way, 0, part].astype(F32)
        if part == F_A:
            links.arrive(("last",), frecv, across)
            value = value + frecv[...].astype(F32)
        mixed_v[:, cols] = value.astype(BF16)
    store(mixed_v, mixed_hbm)

    links.drain()
    for copy in stores:
        copy.wait()


def fused(sizes, residual, gate_t, up_t, w, cot, outer, deltas, momentum, partner):
    nxh, nz, ny = sizes
    width = w.shape[1]
    half, far = width // 2, ny // 2
    anywhere = pl.BlockSpec(memory_space=pl.ANY)
    count = message_count(ny, nz, nxh)
    shapes = (residual, gate_t, up_t, w, outer, outer)
    slabs = (2, ny, 8, width)
    scratch = [
        pltpu.VMEM(residual.shape, BF16),
        pltpu.VMEM(gate_t.shape, BF16),
        pltpu.VMEM(gate_t.shape, BF16),
        pltpu.VMEM(w.shape, BF16),
        pltpu.VMEM((4 * ny, 8, width), BF16),
        pltpu.VMEM(outer.shape, F32),
        pltpu.VMEM(outer.shape, F32),
        pltpu.VMEM(outer.shape, F32),
        pltpu.SMEM(partner.shape, jnp.int32),
        pltpu.VMEM(gate_t.shape, BF16),
        pltpu.VMEM((2, 2 * ny * 8, gate_t.shape[0]), BF16),
        pltpu.VMEM(gate_t.shape, F32),
        pltpu.VMEM(gate_t.shape, F32),
        pltpu.VMEM(slabs, F32),
        pltpu.VMEM(slabs, BF16),
        pltpu.VMEM(slabs, BF16),
        pltpu.VMEM((ny, 8, half), BF16),
        pltpu.VMEM((ny, 8, half), BF16),
        pltpu.VMEM((2, far, 3, 8, half), BF16),
        pltpu.VMEM((2, far, 3, 8, half), BF16),
        pltpu.VMEM((8, half), BF16),
        pltpu.VMEM((8, half), BF16),
        pltpu.VMEM((nz,) + outer.shape, BF16),
        pltpu.VMEM((nxh,) + outer.shape, BF16),
        pltpu.VMEM((nxh,) + outer.shape, BF16),
        pltpu.VMEM(residual.shape, BF16),
        pltpu.VMEM(gate_t.shape, BF16),
        pltpu.VMEM(gate_t.shape, BF16),
        pltpu.VMEM(w.shape, BF16),
        pltpu.VMEM(outer.shape, F32),
        pltpu.VMEM(outer.shape, F32),
        pltpu.SemaphoreType.DMA((9,)),
        pltpu.SemaphoreType.DMA((7,)),
        pltpu.SemaphoreType.DMA((count,)),
        pltpu.SemaphoreType.DMA((count,)),
    ]
    return pl.pallas_call(
        functools.partial(kernel, sizes),
        name="layer",
        out_shape=[jax.ShapeDtypeStruct(a.shape, a.dtype) for a in shapes],
        in_specs=[anywhere] * 9,
        out_specs=[anywhere] * 6,
        scratch_shapes=scratch,
        compiler_params=pltpu.CompilerParams(
            collective_id=0, has_side_effects=True, vmem_limit_bytes=60 * 1024 * 1024
        ),
    )(residual, gate_t, up_t, w, cot, outer, deltas, momentum, partner)


def per_device(
    sizes, residual, gate_pre, up_pre, w, cotangent, outer_weights, deltas, momentum, partner
):
    flat = (outer_weights.shape[1] // 128, 128)
    mixed, grad_gate, grad_up, grad_down, new_outer, new_momentum = fused(
        sizes,
        residual[0],
        gate_pre[0].T,
        up_pre[0].T,
        w,
        cotangent[0],
        outer_weights.reshape(flat),
        deltas.reshape(flat),
        momentum.reshape(flat),
        partner,
    )
    return (
        mixed[None],
        grad_gate.T[None],
        grad_up.T[None],
        grad_down[None],
        new_outer.reshape(outer_weights.shape),
        new_momentum.reshape(outer_weights.shape),
    )


def build(devices, sizes):
    nxh, nz, ny = sizes
    torus = Mesh(devices.reshape(nxh, nz, ny, 2, 2), ISLAND + TP)
    return jax.shard_map(
        functools.partial(per_device, sizes),
        mesh=torus,
        in_specs=(
            P(ISLAND, TP, None),
            P(ISLAND, None, TP),
            P(ISLAND, None, TP),
            P(TP, None),
            P(ISLAND, TP, None),
            P(ISLAND, TP),
            P(ISLAND, TP),
            P(ISLAND, TP),
            P(),
        ),
        out_specs=(
            P(ISLAND, TP, None),
            P(ISLAND, None, TP),
            P(ISLAND, None, TP),
            P(ISLAND, TP, None),
            P(ISLAND, TP),
            P(ISLAND, TP),
        ),
        check_vma=False,
    )


def solution(mesh):
    return build(mesh.devices, (4, 8, mesh.shape["tp"] // 4))
```

time: 132 us -> 59.8 us (0.45)
  Pallas kernels: 0 us -> 49.4 us
  waiting for transfers between devices: 44.1 us -> 0 us
  blocking collectives: 40.5 us -> 0 us
  starting transfers between devices: 18.6 us -> 0 us
  between operations: 14.1 us -> 0.65 us
  matrix products: 8.17 us -> 0 us
  local copies, waits for them, and re-layouts: 1.68 us -> 8.74 us
  other arithmetic: 4.85 us -> 0 us
    pallas_call x0 -> x1, Pallas kernels: none -> 49.4 us  [fused(): pl.pallas_call(functools.partial(kernel, sizes), name='layer', out_shape=...]
    all_gather x2 -> x0, blocking collectives: 40.5 us -> none  [stacked_from(): parts = lax.all_gather(parts, axes[k])]
    all_gather x1 -> x0, waiting for transfers between devices: 27.9 us -> none  [per_device(): piece = lax.all_gather(cotangent, 'tp', axis=0, tiled=True)]
    all_to_all x1 -> x0, starting transfers between devices: 18.6 us -> none  [summed_on_arrival(): lax.all_to_all(parts, axis, split_axis=0, concat_axis=0, tiled=True)]
    all_to_all x1 -> x0, waiting for transfers between devices: 15.5 us -> none  [summed_on_arrival(): lax.all_to_all(parts, axis, split_axis=0, concat_axis=0, tiled=True)]
    dot_general x3 -> x0, matrix products: 8.17 us -> none  [the longest x1 3.22 us: per_device(): lax.dot_general(piece, down_weight, (((1,), (1,)), ((), ())), preferred_e...]
    unnamed x19 -> x10, local copies, waits for them, and re-layouts: 1.68 us -> 8.74 us
    reduce_sum x3 -> x0, other arithmetic: 2.76 us -> none  [the longest x1 1.9 us: summed_on_arrival(): return arrived.astype(jnp.float32).sum(axis=0)]
  transfers between devices with their start and end apart: 2 -> 0, of which waited for: 2 -> 0; matrix products, arithmetic and copies ran while one was open for 4% -> 0% of each run, Pallas kernels for 0% -> 0%
where the time goes in v1:
time: 59.8 us; the launch traced here: 58.8 us
  Pallas kernels  49.4 us (83%)
  local copies, waits for them, and re-layouts  8.74 us (15%)
  between operations  0.65 us (1%)
    pallas_call x1, Pallas kernels, fused(): pl.pallas_call(functools.partial(kernel, sizes), name='layer', out_shape=...  49.4 us
    unnamed x10, local copies, waits for them, and re-layouts  8.74 us

profile of v1, /device:TPU:1, one launch (start us, length us, event | category | flops | bytes accessed | tf_op | source)
XLA Modules:
  0.0 58.8 jit_solution(14468441836442444990)
XLA Ops:
  0.6 49.4 %layer.1 = (bf16[8,4096]{1,0:T(8,128)(2,1)}, bf16[224,256]{1,0:T(8,128)(2,1)}, bf16[224,256]{1,0:T(8,128)(2,1)}, bf16[224,4096]{1,0:T(8,128)(2,1)}, f32[64,128]{1,0:T(8,128)}, /*index=5*/f32[64,128]{1,0:T(8,128)}) custom-call(bf16[8,4096]{1,0:T(8,128)(2,1)} %bitcast.26, bf16[224,256]{1,0:T(8,128)(2,1)} %bitcast.24, bf16[224,256]{1,0:T(8,128)(2,1)} %bitcast.25, ...), custom_call_target="tpu_custom_call" | custom-call | tf_op jit(solution)/shard_map/layer/pallas_call | solution.py:498
  50.1 1.5 %copy.21 = bf16[1,8,4096]{2,1,0:T(8,128)(2,1)} copy(bf16[1,8,4096]{2,1,0:T(8,128)(2,1)} %bitcast.28) | data formatting | bytes 131072
  51.5 1.6 %copy.22 = bf16[1,256,224]{1,2,0:T(8,128)(2,1)} copy(bf16[1,256,224]{1,2,0:T(8,128)(2,1)} %bitcast.23) | data formatting | bytes 229376
  53.1 1.6 %copy.23 = bf16[1,256,224]{1,2,0:T(8,128)(2,1)} copy(bf16[1,256,224]{1,2,0:T(8,128)(2,1)} %bitcast.22) | data formatting | bytes 229376
  54.6 0.0 copy-start.1
  54.6 0.0 copy-start
  54.6 2.9 %copy.24 = bf16[1,224,4096]{2,1,0:T(8,128)(2,1)} copy(bf16[1,224,4096]{2,1,0:T(8,128)(2,1)} %bitcast.21) | data formatting | bytes 3670016
  57.6 0.0 copy-done.1
  57.6 0.6 %copy.25 = f32[1,8192]{1,0:T(1,128)} copy(f32[1,8192]{1,0:T(1,128)S(1)} %bitcast.33) | data formatting | bytes 65536
  58.2 0.0 copy-done
  58.2 0.6 %copy.26 = f32[1,8192]{1,0:T(1,128)} copy(f32[1,8192]{1,0:T(1,128)S(1)} %bitcast.32) | data formatting | bytes 65536
Async XLA Ops:
  54.6 2.9 %copy-start.1 = (f32[64,128]{1,0:T(8,128)S(1)}, f32[64,128]{1,0:T(8,128)}, u32[]{:S(2)}) copy-start(f32[64,128]{1,0:T(8,128)} %get-tuple-element.16) | copy-start | bytes 98308
  54.6 3.5 %copy-start = (f32[64,128]{1,0:T(8,128)S(1)}, f32[64,128]{1,0:T(8,128)}, u32[]{:S(2)}) copy-start(f32[64,128]{1,0:T(8,128)} %get-tuple-element.17) | copy-start | bytes 98308
